TPU v7x, 256 devices: a whole 4x4x8 slice. The times are simulated.
256 devices in a mesh: task: 4 (over z_lo), tile: 64 (over y, z_hi, x, core).
Axes of the slice: x: 4, y: 4, z: 8 (z_hi: 2, z_lo: 4; z = z_hi * 4 + z_lo), core: 2. Of those that a mesh axis runs over, the one named last changes fastest.
Arguments:
- adjusted: bfloat16 [8, 3584, 18944], P('task', 'tile'), may hold values from -6 to 6
- fisher: bfloat16 [8, 3584, 18944], P('task', 'tile'), may hold values from 0.0099487305 to 10
Outputs:
- merged: bfloat16 [3584, 18944], P(None, ('task', 'tile'))
All inputs are finite; a program needn't handle non-finite values.
Results may differ from a plain program's by a relative error of at most 0.001.
Values may be sent and summed in bfloat16 or wider, within the bound.
No kernel may reach another device: no remote copies, remote signals or barrier semaphores. Data moves between devices by JAX's collectives and lax.ppermute only.
A program may use at most 64 MiB of HBM per device.

v0:
```python
import jax
import jax.numpy as jnp
from jax import lax
from jax.sharding import PartitionSpec as P


def in_one_piece(arrays, axis, dim, along):
    both = jnp.concatenate(arrays, axis=along)
    out, at, outs = (lax.psum_scatter(both, axis, scatter_dimension=dim, tiled=True), 0, [])
    for a in arrays:
        outs.append(lax.slice_in_dim(out, at, at + a.shape[along], axis=along))
        at += a.shape[along]
    return tuple(outs)


def body(adjusted, fisher):
    scaled = fisher.astype(jnp.float32)
    numerator = jnp.sum(scaled * adjusted.astype(jnp.float32), axis=0)
    denominator = jnp.sum(scaled, axis=0)
    summed_num, summed_den = in_one_piece((numerator, denominator), "task", 1, 0)
    owner_num, owner_den = (
        lax.all_to_all(summed_num, "tile", split_axis=1, concat_axis=0, tiled=True),
        lax.all_to_all(summed_den, "tile", split_axis=1, concat_axis=0, tiled=True),
    )
    merged = (owner_num / owner_den).astype(jnp.bfloat16)
    return merged


def solution(mesh):
    return jax.shard_map(
        body,
        mesh=mesh,
        in_specs=(P("task", "tile", None), P("task", "tile", None)),
        out_specs=P(None, ("task", "tile")),
        check_vma=False,
    )
```

profile of v0, /device:TPU:65, one launch (start us, length us, event | category | flops | bytes accessed | tf_op | source)
XLA Modules:
  0.0 302.0 jit_solution(2950465631684679464)
XLA Ops:
  6.5 0.0 reduce-scatter.2.cloned.1.call-start
  6.5 6.1 %fusion = (f32[56,18944]{1,0:T(8,128)S(1)}, f32[56,18944]{1,0:T(8,128)S(1)}) fusion(bf16[2,56,18944]{2,1,0:T(8,128)(2,1)} %param.3, bf16[2,56,18944]{2,1,0:T(8,128)(2,1)} %param.2), kind=kLoop, calls=%fused_computation.2 | loop fusion | flops 8486912 | bytes 16973824 | tf_op jit(solution)/shard_map/reduce_sum | solution.py:18
  12.6 3.8 %pad_maximum_fusion = f32[112,18944]{1,0:T(8,128)} fusion(f32[56,18944]{1,0:T(8,128)S(1)} %get-tuple-element.6, f32[56,18944]{1,0:T(8,128)S(1)} %get-tuple-element.5), kind=kLoop, calls=%fused_computation.3 | loop fusion | flops 2121728 | bytes 16973824 | tf_op jit(solution)/shard_map/concatenate | solution.py:8
  16.4 0.0 reduce-scatter.2.cloned.1.call-update
  16.5 154.7 %reduce-scatter.2.cloned.1.call-done = f32[112,4736]{1,0:T(8,128)} async-done(((f32[112,18944]{1,0:T(8,128)}), f32[112,4736]{1,0:T(8,128)}) %reduce-scatter.2.cloned.1.call-update) | async-done | bytes 2121744 | tf_op jit(solution)/shard_map/reduce_scatter | solution.py:9
  171.1 2.7 fusion.1
  173.8 4.0 %all_to_all.22 = f32[56,64,74]{2,1,0:T(8,128)S(1)} reshape(f32[56,4736]{1,0:T(8,128)} %get-tuple-element.7) | data formatting | bytes 2121728 | tf_op jit(solution)/shard_map/all_to_all | solution.py:23
  177.8 2.3 copy.6
  180.1 10.5 %all-to-all-start.1 = ((f32[56,64,74]{2,0,1:T(8,128)}), f32[56,64,74]{2,0,1:T(8,128)S(1)}, u32[]{:S(2)}, u32[]{:S(2)}) async-start(f32[56,64,74]{2,0,1:T(8,128)} %copy.6), calls=%async_computation.2 | async-start | bytes 3670016 | tf_op jit(solution)/shard_map/all_to_all | solution.py:23
  190.6 4.1 %all_to_all.20 = f32[56,64,74]{2,1,0:T(8,128)} reshape(f32[56,4736]{1,0:T(8,128)S(1)} %get-tuple-element.8) | data formatting | bytes 2121728 | tf_op jit(solution)/shard_map/all_to_all | solution.py:22
  194.7 3.8 %copy.5 = f32[56,64,74]{2,0,1:T(8,128)} copy(f32[56,64,74]{2,1,0:T(8,128)} %all_to_all.20) | data formatting | bytes 2121728 | tf_op jit(solution)/shard_map/all_to_all | solution.py:22
  198.5 41.8 %all-to-all-done.1 = f32[56,64,74]{2,0,1:T(8,128)S(1)} async-done(((f32[56,64,74]{2,0,1:T(8,128)}), f32[56,64,74]{2,0,1:T(8,128)S(1)}, u32[]{:S(2)}, u32[]{:S(2)}) %all-to-all-start.1) | async-done | bytes 1060896 | tf_op jit(solution)/shard_map/all_to_all | solution.py:23
  240.3 53.2 %all_to_all.26 = f32[56,64,74]{2,0,1:T(8,128)S(1)} all-to-all(f32[56,64,74]{2,0,1:T(8,128)} %copy.5), channel_id=1, replica_groups=mesh['task'=4,'tile'=64] {'tile'}, dimensions={1} | all-to-all | bytes 2121728 | tf_op jit(solution)/shard_map/all_to_all | solution.py:22
  293.5 0.4 divide_convert_fusion
  294.0 1.2 copy.7
Async XLA Ops:
  6.5 164.6 %reduce-scatter.2.cloned.1.call-start = ((), (), s32[]{:S(2)}) async-start(), calls=%async_computation.3 | async-start | bytes 10608640 | tf_op jit(solution)/shard_map/reduce_scatter | solution.py:9
  180.1 60.2 %all-to-all-start.1 = ((f32[56,64,74]{2,0,1:T(8,128)}), f32[56,64,74]{2,0,1:T(8,128)S(1)}, u32[]{:S(2)}, u32[]{:S(2)}) async-start(f32[56,64,74]{2,0,1:T(8,128)} %copy.6), calls=%async_computation.2 | async-start | bytes 3670016 | tf_op jit(solution)/shard_map/all_to_all | solution.py:23
Sparse Core Ops, SparseCore 0:
  16.6 154.4 reduce-scatter.1
where the time goes:
time: 302 us
  waiting for transfers between devices  196 us (65%)
  blocking collectives  53.2 us (18%)
  local copies, waits for them, and re-layouts  18.1 us (6%)
  between operations  13.4 us (4%)
  starting transfers between devices  10.5 us (3%)
  other arithmetic  10.3 us (3%)
    reduce_scatter x1, waiting for transfers between devices, in_one_piece(): lax.psum_scatter(both, axis, scatter_dimension=dim, tiled=True)  155 us
    all_to_all x1, blocking collectives, body(): lax.all_to_all(summed_num, 'tile', split_axis=1, concat_axis=0, tiled=True)  53.2 us
    all_to_all x1, waiting for transfers between devices, body(): lax.all_to_all(summed_den, 'tile', split_axis=1, concat_axis=0, tiled=True)  41.8 us
    all_to_all x1, starting transfers between devices, body(): lax.all_to_all(summed_den, 'tile', split_axis=1, concat_axis=0, tiled=True)  10.5 us
    all_to_all x2, local copies, waits for them, and re-layouts, body(): lax.all_to_all(summed_num, 'tile', split_axis=1, concat_axis=0, tiled=True)  7.92 us
    all_to_all x2, local copies, waits for them, and re-layouts, body(): lax.all_to_all(summed_den, 'tile', split_axis=1, concat_axis=0, tiled=True)  6.32 us
    reduce_sum x1, other arithmetic, body(): numerator = jnp.sum(scaled * adjusted.astype(jnp.float32), axis=0)  6.06 us
  transfers between devices with their start and end apart: 2, of which 2 were waited for; matrix products, arithmetic and copies ran while one was open for 1% of the time, Pallas kernels for 0%

commit v1 on v0

v1 whole, which is shorter than its diff:
```python
import functools

import jax
import jax.numpy as jnp
from jax import lax
from jax.experimental import pallas as pl
from jax.experimental.pallas import tpu as pltpu
from jax.sharding import PartitionSpec as P

ROWS = (56,)
LANES = 128
SUB = 8

TOP = 6.0
M_SCALE = 251.0 / TOP
M_BASE = -125.0
LOG_LOW = -6.0
LOG_HIGH = 6.5
D_SCALE = 250.0 / (LOG_HIGH - LOG_LOW)
D_BASE = -125.0 - D_SCALE * LOG_LOW


def encode(n, d):
    m = n / d
    y = jnp.exp2(jnp.abs(m) * M_SCALE + M_BASE)
    y = jnp.where(m < 0, -y, y)
    z = jnp.exp2(jnp.log2(d) * D_SCALE + D_BASE)
    return y.astype(jnp.bfloat16), z.astype(jnp.bfloat16)


def decode(y, z):
    y = y.astype(jnp.float32)
    m = (jnp.log2(jnp.abs(y)) - M_BASE) * (1.0 / M_SCALE)
    m = jnp.where(y < 0, -m, m)
    d = jnp.exp2((jnp.log2(z.astype(jnp.float32)) - D_BASE) * (1.0 / D_SCALE))
    return m * d, d


def local(a_ref, f_ref, at):
    n = d = None
    for m in range(a_ref.shape[0]):
        f = f_ref[m, :, at].astype(jnp.float32)
        p = f * a_ref[m, :, at].astype(jnp.float32)
        n, d = (p, f) if n is None else (n + p, d + f)
    return n, d


def tiles(width):
    return [slice(c, c + LANES) for c in range(0, width, LANES)]


def first_kernel(q_ref, a_ref, f_ref, o_ref):
    for at in tiles(a_ref.shape[2]):
        o_ref[0, 0, :, at], o_ref[0, 1, :, at] = encode(*local(a_ref, f_ref, at))


def second_kernel(q_ref, a_ref, f_ref, r_ref, o_ref):
    for at in tiles(a_ref.shape[2]):
        n, d = local(a_ref, f_ref, at)
        rn, rd = decode(r_ref[0, 0, :, at], r_ref[0, 1, :, at])
        o_ref[0, :, at], o_ref[1, :, at] = encode(n + rn, d + rd)


def third_kernel(q_ref, a_ref, f_ref, r_ref, s_ref, o_ref, w_ref):
    for at in tiles(a_ref.shape[2]):
        n, d = local(a_ref, f_ref, at)
        rn, rd = decode(r_ref[0, 0, :, at], r_ref[0, 1, :, at])
        sn, sd = decode(s_ref[0, :, at], s_ref[1, :, at])
        w_ref[:, at] = (n + rn + sn) / (d + rd + sd)
    peers, _, cols = o_ref.shape
    for j in range(peers):
        o_ref[j] = w_ref[:, j * cols : (j + 1) * cols].astype(jnp.bfloat16)


def call(kernel, grid, quarters, in_specs, out_specs, out_shape, scratch, *args):
    return pl.pallas_call(
        kernel,
        grid_spec=pltpu.PrefetchScalarGridSpec(
            num_scalar_prefetch=1, grid=grid, in_specs=in_specs, out_specs=out_specs, scratch_shapes=scratch
        ),
        out_shape=out_shape,
    )(quarters, *args)


def body(tile, adjusted, fisher):
    models, rows, width = adjusted.shape
    part = width // 4
    bf16 = jnp.bfloat16
    t = lax.axis_index("task")
    pick = lambda *xs: jnp.stack([t ^ x for x in xs]).astype(jnp.int32)
    outs, start = [], 0
    for r in ROWS:
        at = start // SUB
        start += r
        n = r // SUB
        raw2 = pl.BlockSpec((models, SUB, part), lambda s, i, q, at=at: (0, at + i, q[s]))
        raw1 = pl.BlockSpec((models, SUB, part), lambda i, q, at=at: (0, at + i, q[0]))
        pair = pl.BlockSpec((2, SUB, part), lambda i, q: (0, i, 0))
        slot = lambda k: pl.BlockSpec((1, 2, SUB, part), lambda i, q: (k, 0, i, 0))
        sent = call(
            first_kernel, (2, n), pick(1, 3), [raw2, raw2],
            pl.BlockSpec((1, 2, SUB, part), lambda s, i, q: (s, 0, i, 0)),
            jax.ShapeDtypeStruct((2, 2, r, part), bf16), [], adjusted, fisher,
        )
        got = lax.ppermute(sent, "task", [(k, k ^ 1) for k in range(4)])
        sent = call(
            second_kernel, (n,), pick(2), [raw1, raw1, slot(1)], pair,
            jax.ShapeDtypeStruct((2, r, part), bf16), [], adjusted, fisher, got,
        )
        last = lax.ppermute(sent, "task", [(k, k ^ 2) for k in range(4)])
        cols = part // tile
        merged = call(
            third_kernel, (n,), pick(0), [raw1, raw1, slot(0), pair],
            pl.BlockSpec((tile, SUB, cols), lambda i, q: (0, i, 0)),
            jax.ShapeDtypeStruct((tile, r, cols), bf16), [pltpu.VMEM((SUB, part), jnp.float32)],
            adjusted, fisher, got, last,
        )
        outs.append(lax.all_to_all(merged, "tile", 0, 0, tiled=True))
    out = jnp.concatenate(outs, axis=1) if len(outs) > 1 else outs[0]
    return out.reshape(tile * rows, part // tile)


def solution(mesh):
    return jax.shard_map(
        functools.partial(body, mesh.shape["tile"]),
        mesh=mesh,
        in_specs=(P("task", "tile", None), P("task", "tile", None)),
        out_specs=P(None, ("task", "tile")),
        check_vma=False,
    )
```

time: 302 us -> 167 us (0.55)
  the two profiles are of different devices: /device:TPU:65 before, /device:TPU:1 now
where the time goes in v1:
time: 167 us
  waiting for transfers between devices  91 us (54%)
  blocking collectives  42.4 us (25%)
  Pallas kernels  22.9 us (14%)
  starting transfers between devices  6.25 us (4%)
  local copies, waits for them, and re-layouts  3.51 us (2%)
    ppermute x1, waiting for transfers between devices, body(): last = lax.ppermute(sent, 'task', [(k, k ^ 2) for k in range(4)])  45.8 us
    ppermute x1, waiting for transfers between devices, body(): got = lax.ppermute(sent, 'task', [(k, k ^ 1) for k in range(4)])  45.2 us
    all_to_all x1, blocking collectives, body(): outs.append(lax.all_to_all(merged, 'tile', 0, 0, tiled=True))  42.4 us
    pallas_call x3, Pallas kernels, call(): pl.pallas_call(kernel, grid_spec=pltpu.PrefetchScalarGridSpec(num_scalar_...  22.9 us
    ppermute x1, starting transfers between devices, body(): last = lax.ppermute(sent, 'task', [(k, k ^ 2) for k in range(4)])  3.79 us
  transfers between devices with their start and end apart: 2, of which 2 were waited for; matrix products, arithmetic and copies ran while one was open for 0% of the time, Pallas kernels for 0%

profile of v1, /device:TPU:1, one launch (start us, length us, event | category | flops | bytes accessed | tf_op | source)
XLA Modules:
  0.0 166.6 jit_solution(17931380004656948186)
XLA Ops:
  0.0 0.6 pad_add_fusion.q_ref
  0.6 10.4 %shard_map.28 = bf16[2,2,56,4736]{3,2,1,0:T(8,128)(2,1)} custom-call(s32[2]{0:T(128)} %pad_add_fusion.q_ref, bf16[2,56,18944]{2,1,0:T(8,128)(2,1)} %a_ref.5, bf16[2,56,18944]{2,1,0:T(8,128)(2,1)} %f_ref.5), custom_call_target="tpu_custom_call" | custom-call | tf_op jit(solution)/shard_map/pallas_call | solution.py:76
  11.0 2.5 %collective-permute-start = (bf16[2,2,56,4736]{3,2,1,0:T(8,128)(2,1)}, bf16[2,2,56,4736]{3,2,1,0:T(8,128)(2,1)S(1)}, u32[]{:S(2)}, u32[]{:S(2)}) collective-permute-start(bf16[2,2,56,4736]{3,2,1,0:T(8,128)(2,1)} %shard_map.28), channel_id=1, source_target_pairs={{0,64},{64,0},{128,192},{192,128},{1,65},{65,1},{129,193},{193,129... | collective-permute-start | bytes 6365192 | tf_op jit(solution)/shard_map/ppermute | solution.py:105
  13.4 45.2 %collective-permute-done.r_ref = bf16[2,2,56,4736]{3,2,1,0:T(8,128)(2,1)S(1)} collective-permute-done((bf16[2,2,56,4736]{3,2,1,0:T(8,128)(2,1)}, bf16[2,2,56,4736]{3,2,1,0:T(8,128)(2,1)S(1)}, u32[]{:S(2)}, u32[]{:S(2)}) %collective-permute-start) | collective-permute-done | bytes 2121760 | tf_op jit(solution)/shard_map/ppermute | solution.py:105
  58.6 0.0 copy-start
  58.6 1.3 copy-done
  59.9 6.0 %shard_map.29 = bf16[2,56,4736]{2,1,0:T(8,128)(2,1)} custom-call(s32[1]{0:T(128)} %bitcast.3.q_ref, bf16[2,56,18944]{2,1,0:T(8,128)(2,1)} %a_ref.5, bf16[2,56,18944]{2,1,0:T(8,128)(2,1)} %f_ref.5, bf16[2,2,56,4736]{3,2,1,0:T(8,128)(2,1)} %copy-done), custom_call_target="tpu_custom_call" | custom-call | tf_op jit(solution)/shard_map/pallas_call | solution.py:76
  65.9 3.8 %collective-permute-start.1 = (bf16[2,56,4736]{2,1,0:T(8,128)(2,1)}, bf16[2,56,4736]{2,1,0:T(8,128)(2,1)S(1)}, u32[]{:S(2)}, u32[]{:S(2)}) collective-permute-start(bf16[2,56,4736]{2,1,0:T(8,128)(2,1)} %shard_map.29), channel_id=1, source_target_pairs={{0,128},{64,192},{128,0},{192,64},{1,129},{65,193},{129,1},{193,65... | collective-permute-start | bytes 3182600 | tf_op jit(solution)/shard_map/ppermute | solution.py:110
  69.7 45.8 %collective-permute-done.1.s_ref = bf16[2,56,4736]{2,1,0:T(8,128)(2,1)S(1)} collective-permute-done((bf16[2,56,4736]{2,1,0:T(8,128)(2,1)}, bf16[2,56,4736]{2,1,0:T(8,128)(2,1)S(1)}, u32[]{:S(2)}, u32[]{:S(2)}) %collective-permute-start.1) | collective-permute-done | bytes 1060896 | tf_op jit(solution)/shard_map/ppermute | solution.py:110
  115.5 0.0 copy-start.1
  115.5 1.0 copy-done.1
  116.5 6.5 %shard_map.30 = bf16[64,56,74]{2,1,0:T(8,128)(2,1)} custom-call(s32[1]{0:T(128)} %bitcast.q_ref, bf16[2,56,18944]{2,1,0:T(8,128)(2,1)} %a_ref.5, bf16[2,56,18944]{2,1,0:T(8,128)(2,1)} %f_ref.5, bf16[2,2,56,4736]{3,2,1,0:T(8,128)(2,1)} %copy-done, bf16[2,56,4736]{2,1,0:T(8,128)(2,1)} %copy-done.1), custom_call_target="tpu_custom_call" | custom-call | tf_op jit(solution)/shard_map/pallas_call | solution.py:76
  123.1 42.4 %all_to_all.5 = bf16[64,56,74]{2,1,0:T(8,128)(2,1)S(1)} all-to-all(bf16[64,56,74]{2,1,0:T(8,128)(2,1)} %shard_map.30), channel_id=1, replica_groups=mesh['task'=4,'tile'=64] {'tile'}, dimensions={0} | all-to-all | bytes 1060864 | tf_op jit(solution)/shard_map/all_to_all | solution.py:118
  165.4 1.2 copy.3
Async XLA Ops:
  11.0 47.6 %collective-permute-start = (bf16[2,2,56,4736]{3,2,1,0:T(8,128)(2,1)}, bf16[2,2,56,4736]{3,2,1,0:T(8,128)(2,1)S(1)}, u32[]{:S(2)}, u32[]{:S(2)}) collective-permute-start(bf16[2,2,56,4736]{3,2,1,0:T(8,128)(2,1)} %shard_map.28), channel_id=1, source_target_pairs={{0,64},{64,0},{128,192},{192,128},{1,65},{65,1},{129,193},{193,129... | collective-permute-start | bytes 6365192 | tf_op jit(solution)/shard_map/ppermute | solution.py:105
  58.6 1.3 copy-start
  65.9 49.6 %collective-permute-start.1 = (bf16[2,56,4736]{2,1,0:T(8,128)(2,1)}, bf16[2,56,4736]{2,1,0:T(8,128)(2,1)S(1)}, u32[]{:S(2)}, u32[]{:S(2)}) collective-permute-start(bf16[2,56,4736]{2,1,0:T(8,128)(2,1)} %shard_map.29), channel_id=1, source_target_pairs={{0,128},{64,192},{128,0},{192,64},{1,129},{65,193},{129,1},{193,65... | collective-permute-start | bytes 3182600 | tf_op jit(solution)/shard_map/ppermute | solution.py:110
  115.5 1.0 copy-start.1

commit v2 on v1

v2 whole, which is shorter than its diff:
```python
import functools

import jax
import jax.numpy as jnp
from jax import lax
from jax.experimental import pallas as pl
from jax.experimental.pallas import tpu as pltpu
from jax.sharding import Mesh, PartitionSpec as P

ROWS = (24, 16, 16)
LANES = 128
SUB = 8
TILE = (("y", 4), ("half", 2), ("x", 4), ("core", 2))
PLANE = ("y", "x", "core")

TOP = 6.0
M_SCALE = 251.0 / TOP
M_BASE = -125.0
LOG_LOW = -6.0
LOG_HIGH = 6.5
D_SCALE = 250.0 / (LOG_HIGH - LOG_LOW)
D_BASE = -125.0 - D_SCALE * LOG_LOW


def encode(n, d):
    m = n / d
    y = jnp.exp2(jnp.abs(m) * M_SCALE + M_BASE)
    y = jnp.where(m < 0, -y, y)
    z = jnp.exp2(jnp.log2(d) * D_SCALE + D_BASE)
    return y.astype(jnp.bfloat16), z.astype(jnp.bfloat16)


def decode(y, z):
    y = y.astype(jnp.float32)
    m = (jnp.log2(jnp.abs(y)) - M_BASE) * (1.0 / M_SCALE)
    m = jnp.where(y < 0, -m, m)
    d = jnp.exp2((jnp.log2(z.astype(jnp.float32)) - D_BASE) * (1.0 / D_SCALE))
    return m * d, d


def sums(refs, segment, c):
    at = slice(c, c + LANES)
    first, last = c // segment, (c + LANES - 1) // segment

    def load(k, m):
        two = [refs[2 * (s % 2) + k][m, :, at].astype(jnp.float32) for s in sorted({first, last})]
        if len(two) == 1:
            return two[0]
        lane = lax.broadcasted_iota(jnp.int32, two[0].shape, 1)
        return jnp.where(lane < last * segment - c, two[0], two[1])

    n = d = None
    for m in range(refs[0].shape[0]):
        f = load(1, m)
        p = f * load(0, m)
        n, d = (p, f) if n is None else (n + p, d + f)
    return at, n, d


def first_kernel(segment, q_ref, a0, f0, a1, f1, o_ref):
    for c in range(0, a0.shape[2], LANES):
        at, n, d = sums((a0, f0, a1, f1), segment, c)
        o_ref[0, 0, :, at], o_ref[0, 1, :, at] = encode(n, d)


def second_kernel(segment, q_ref, a0, f0, a1, f1, r_ref, o_ref):
    for c in range(0, a0.shape[2], LANES):
        at, n, d = sums((a0, f0, a1, f1), segment, c)
        rn, rd = decode(r_ref[0, 0, :, at], r_ref[0, 1, :, at])
        o_ref[0, :, at], o_ref[1, :, at] = encode(n + rn, d + rd)


def third_kernel(segment, q_ref, a0, f0, a1, f1, r_ref, s_ref, o_ref, w_ref):
    for c in range(0, a0.shape[2], LANES):
        at, n, d = sums((a0, f0, a1, f1), segment, c)
        rn, rd = decode(r_ref[0, 0, :, at], r_ref[0, 1, :, at])
        sn, sd = decode(s_ref[0, :, at], s_ref[1, :, at])
        w_ref[:, at] = (n + rn + sn) / (d + rd + sd)
    halves, peers, _, cols = o_ref.shape
    per = segment // cols
    for j in range(halves * peers):
        block, k = divmod(j, per)
        to = w_ref[:, j * cols : (j + 1) * cols].astype(jnp.bfloat16)
        o_ref[block % 2, block // 2 * per + k] = to


def call(kernel, grid, quarters, in_specs, out_specs, out_shape, scratch, *args):
    return pl.pallas_call(
        kernel,
        grid_spec=pltpu.PrefetchScalarGridSpec(
            num_scalar_prefetch=1, grid=grid, in_specs=in_specs, out_specs=out_specs, scratch_shapes=scratch
        ),
        out_shape=out_shape,
    )(quarters, *args)


def body(adjusted, fisher):
    models, rows, width = adjusted.shape
    part = width // 4
    bf16 = jnp.bfloat16
    sizes = dict(TILE)
    peers = sizes["y"] * sizes["x"] * sizes["core"]
    cols = part // (2 * peers)
    segment = cols * sizes["x"] * sizes["core"]
    t = lax.axis_index("task")
    half = lax.axis_index("half")
    pick = lambda *xs: jnp.stack([t ^ x ^ jnp.where(half == h, 0, 3) for x in xs for h in (0, 1)]).astype(jnp.int32)
    raw = (adjusted, fisher, adjusted, fisher)
    outs, start = [], 0
    for r in ROWS:
        at = start // SUB
        start += r
        n = r // SUB
        raw2 = lambda k: pl.BlockSpec((models, SUB, part), lambda s, i, q: (0, at + i, q[2 * s + k]))
        raw1 = lambda k: pl.BlockSpec((models, SUB, part), lambda i, q: (0, at + i, q[k]))
        raws1 = [raw1(0), raw1(0), raw1(1), raw1(1)]
        pair = pl.BlockSpec((2, SUB, part), lambda i, q: (0, i, 0))
        slot = lambda k: pl.BlockSpec((1, 2, SUB, part), lambda i, q: (k, 0, i, 0))
        sent = call(
            functools.partial(first_kernel, segment), (2, n), pick(1, 3), [raw2(0), raw2(0), raw2(1), raw2(1)],
            pl.BlockSpec((1, 2, SUB, part), lambda s, i, q: (s, 0, i, 0)),
            jax.ShapeDtypeStruct((2, 2, r, part), bf16), [], *raw,
        )
        got = lax.ppermute(sent, "task", [(k, k ^ 1) for k in range(4)])
        sent = call(
            functools.partial(second_kernel, segment), (n,), pick(2), [*raws1, slot(1)], pair,
            jax.ShapeDtypeStruct((2, r, part), bf16), [], *raw, got,
        )
        last = lax.ppermute(sent, "task", [(k, k ^ 2) for k in range(4)])
        merged = call(
            functools.partial(third_kernel, segment), (n,), pick(0), [*raws1, slot(0), pair],
            pl.BlockSpec((2, peers, SUB, cols), lambda i, q: (0, 0, i, 0)),
            jax.ShapeDtypeStruct((2, peers, r, cols), bf16), [pltpu.VMEM((SUB, part), jnp.float32)],
            *raw, got, last,
        )
        own, other = (lax.select(half == 0, merged[k], merged[1 - k]) for k in (0, 1))
        other = lax.ppermute(other, ("task", "half"), [(2 * u + h, 2 * (u ^ 3) + 1 - h) for u in range(4) for h in (0, 1)])
        both = jnp.stack([lax.select(half == 0, own, other), lax.select(half == 0, other, own)], axis=1)
        outs.append(lax.all_to_all(both, PLANE, 0, 0, tiled=True))
    out = jnp.concatenate(outs, axis=2) if len(outs) > 1 else outs[0]
    out = out.reshape(sizes["y"], sizes["x"] * sizes["core"], 2, rows, cols).transpose(0, 2, 1, 3, 4)
    return out.reshape(2 * peers * rows, cols)


def solution(mesh):
    names, sizes = zip(*TILE)
    fine = Mesh(mesh.devices.reshape(mesh.shape["task"], *sizes), ("task", *names))
    return jax.shard_map(
        body,
        mesh=fine,
        in_specs=(P("task", names, None), P("task", names, None)),
        out_specs=P(None, ("task", *names)),
        check_vma=False,
    )
```

time: 167 us -> 155 us (0.928)
  the two profiles are of different devices: /device:TPU:1 before, /device:TPU:65 now
where the time goes in v2:
time: 155 us; the launch traced here: 154 us
  waiting for transfers between devices  48 us (31%)
  starting transfers between devices  42.1 us (27%)
  Pallas kernels  36.7 us (24%)
  blocking collectives  13.7 us (9%)
  local copies, waits for them, and re-layouts  7.61 us (5%)
  other arithmetic  5.44 us (4%)
    pallas_call x9, Pallas kernels, call(): pl.pallas_call(kernel, grid_spec=pltpu.PrefetchScalarGridSpec(num_scalar_...  36.7 us
    ppermute x3, waiting for transfers between devices, body(): got = lax.ppermute(sent, 'task', [(k, k ^ 1) for k in range(4)])  35.7 us
    ppermute x3, starting transfers between devices, body(): lax.ppermute(other, ('task', 'half'), [(2 * u + h, 2 * (u ^ 3) + 1 - h) f...  20.7 us
    all_to_all x2, starting transfers between devices, body(): outs.append(lax.all_to_all(both, PLANE, 0, 0, tiled=True))  16 us
    all_to_all x1, blocking collectives, body(): outs.append(lax.all_to_all(both, PLANE, 0, 0, tiled=True))  13.7 us
    all_to_all x2, waiting for transfers between devices, body(): outs.append(lax.all_to_all(both, PLANE, 0, 0, tiled=True))  8.66 us
    unnamed x18, local copies, waits for them, and re-layouts  4.84 us
    select_n x3, other arithmetic, body(): lax.select(half == 0, merged[k], merged[1 - k])  3.1 us
  transfers between devices with their start and end apart: 11, of which 5 were waited for; matrix products, arithmetic and copies ran while one was open for 4% of the time, Pallas kernels for 20%

profile of v2, /device:TPU:65, one launch (start us, length us, event | category | flops | bytes accessed | tf_op | source)
XLA Modules:
  0.0 153.7 jit_solution(3759634237829700301)
XLA Ops:
  0.6 5.9 %shard_map.28 = bf16[2,2,24,4736]{3,2,1,0:T(8,128)(2,1)} custom-call(s32[4]{0:T(128)} %pad_add_fusion.1.q_ref, bf16[2,56,18944]{2,1,0:T(8,128)(2,1)} %a1.17, bf16[2,56,18944]{2,1,0:T(8,128)(2,1)} %f1.17, bf16[2,56,18944]{2,1,0:T(8,128)(2,1)} %a1.17, bf16[2,56,18944]{2,1,0:T(8,128)(2,1)} %f1.17), custom_call_target="tpu_custom_call" | custom-call | tf_op jit(solution)/shard_map/pallas_call | solution.py:88
  6.5 1.6 %collective-permute-start = (bf16[2,2,24,4736]{3,2,1,0:T(8,128)(2,1)}, bf16[2,2,24,4736]{3,2,1,0:T(8,128)(2,1)S(1)}, u32[]{:S(2)}, u32[]{:S(2)}) collective-permute-start(bf16[2,2,24,4736]{3,2,1,0:T(8,128)(2,1)} %shard_map.28), channel_id=1, source_target_pairs={{0,64},{64,0},{128,192},{192,128},{1,65},{65,1},{129,193},{193,129... | collective-permute-start | bytes 2727944 | tf_op jit(solution)/shard_map/ppermute | solution.py:124
  8.2 4.5 %shard_map.31 = bf16[2,2,16,4736]{3,2,1,0:T(8,128)(2,1)} custom-call(s32[4]{0:T(128)} %pad_add_fusion.1.q_ref, bf16[2,56,18944]{2,1,0:T(8,128)(2,1)} %a1.17, bf16[2,56,18944]{2,1,0:T(8,128)(2,1)} %f1.17, bf16[2,56,18944]{2,1,0:T(8,128)(2,1)} %a1.17, bf16[2,56,18944]{2,1,0:T(8,128)(2,1)} %f1.17), custom_call_target="tpu_custom_call" | custom-call | tf_op jit(solution)/shard_map/pallas_call | solution.py:88
  12.7 4.5 %shard_map.34 = bf16[2,2,16,4736]{3,2,1,0:T(8,128)(2,1)} custom-call(s32[4]{0:T(128)} %pad_add_fusion.1.q_ref, bf16[2,56,18944]{2,1,0:T(8,128)(2,1)} %a1.17, bf16[2,56,18944]{2,1,0:T(8,128)(2,1)} %f1.17, bf16[2,56,18944]{2,1,0:T(8,128)(2,1)} %a1.17, bf16[2,56,18944]{2,1,0:T(8,128)(2,1)} %f1.17), custom_call_target="tpu_custom_call" | custom-call | tf_op jit(solution)/shard_map/pallas_call | solution.py:88
  17.2 1.5 collective-permute-start.6
  19.3 21.9 %collective-permute-done.3.r_ref = bf16[2,2,16,4736]{3,2,1,0:T(8,128)(2,1)S(1)} collective-permute-done((bf16[2,2,16,4736]{3,2,1,0:T(8,128)(2,1)}, bf16[2,2,16,4736]{3,2,1,0:T(8,128)(2,1)S(1)}, u32[]{:S(2)}, u32[]{:S(2)}) %collective-permute-start.3) | collective-permute-done | bytes 606240 | tf_op jit(solution)/shard_map/ppermute | solution.py:124
  41.2 0.8 copy-done.3
  42.0 3.1 %shard_map.32 = bf16[2,16,4736]{2,1,0:T(8,128)(2,1)} custom-call(s32[2]{0:T(128)} %pad_add_fusion.2.q_ref, bf16[2,56,18944]{2,1,0:T(8,128)(2,1)} %a1.17, bf16[2,56,18944]{2,1,0:T(8,128)(2,1)} %f1.17, bf16[2,56,18944]{2,1,0:T(8,128)(2,1)} %a1.17, bf16[2,56,18944]{2,1,0:T(8,128)(2,1)} %f1.17, bf16[2,2,16,4736]{3,2,1,0:T(8,128)(2,1)} %copy-done.3), custom_call_target="tpu_custom_call" | custom-call | tf_op jit(solution)/shard_map/pallas_call | solution.py:88
  45.0 13.9 %collective-permute-done.6.r_ref = bf16[2,2,16,4736]{3,2,1,0:T(8,128)(2,1)S(1)} collective-permute-done((bf16[2,2,16,4736]{3,2,1,0:T(8,128)(2,1)}, bf16[2,2,16,4736]{3,2,1,0:T(8,128)(2,1)S(1)}, u32[]{:S(2)}, u32[]{:S(2)}) %collective-permute-start.6) | collective-permute-done | bytes 606240 | tf_op jit(solution)/shard_map/ppermute | solution.py:124
  58.9 0.8 copy-done.2
  59.7 3.1 %shard_map.35 = bf16[2,16,4736]{2,1,0:T(8,128)(2,1)} custom-call(s32[2]{0:T(128)} %pad_add_fusion.2.q_ref, bf16[2,56,18944]{2,1,0:T(8,128)(2,1)} %a1.17, bf16[2,56,18944]{2,1,0:T(8,128)(2,1)} %f1.17, bf16[2,56,18944]{2,1,0:T(8,128)(2,1)} %a1.17, bf16[2,56,18944]{2,1,0:T(8,128)(2,1)} %f1.17, bf16[2,2,16,4736]{3,2,1,0:T(8,128)(2,1)} %copy-done.2), custom_call_target="tpu_custom_call" | custom-call | tf_op jit(solution)/shard_map/pallas_call | solution.py:88
  63.5 0.9 copy-done
  64.4 4.3 %shard_map.29 = bf16[2,24,4736]{2,1,0:T(8,128)(2,1)} custom-call(s32[2]{0:T(128)} %pad_add_fusion.2.q_ref, bf16[2,56,18944]{2,1,0:T(8,128)(2,1)} %a1.17, bf16[2,56,18944]{2,1,0:T(8,128)(2,1)} %f1.17, bf16[2,56,18944]{2,1,0:T(8,128)(2,1)} %a1.17, bf16[2,56,18944]{2,1,0:T(8,128)(2,1)} %f1.17, bf16[2,2,24,4736]{3,2,1,0:T(8,128)(2,1)} %copy-done), custom_call_target="tpu_custom_call" | custom-call | tf_op jit(solution)/shard_map/pallas_call | solution.py:88
  68.7 2.4 %collective-permute-start.1 = (bf16[2,24,4736]{2,1,0:T(8,128)(2,1)}, bf16[2,24,4736]{2,1,0:T(8,128)(2,1)S(1)}, u32[]{:S(2)}, u32[]{:S(2)}) collective-permute-start(bf16[2,24,4736]{2,1,0:T(8,128)(2,1)} %shard_map.29), channel_id=1, source_target_pairs={{0,128},{64,192},{128,0},{192,64},{1,129},{65,193},{129,1},{193,65... | collective-permute-start | bytes 1363976 | tf_op jit(solution)/shard_map/ppermute | solution.py:129
  71.1 0.7 copy-done.7
  71.8 3.3 %shard_map.33 = bf16[2,32,16,74]{3,2,1,0:T(8,128)(2,1)} custom-call(s32[2]{0:T(128)} %pad_add_fusion.q_ref, bf16[2,56,18944]{2,1,0:T(8,128)(2,1)} %a1.17, bf16[2,56,18944]{2,1,0:T(8,128)(2,1)} %f1.17, bf16[2,56,18944]{2,1,0:T(8,128)(2,1)} %a1.17, bf16[2,56,18944]{2,1,0:T(8,128)(2,1)} %f1.17, bf16[2,2,16,4736]{3,2,1,0:T(8,128)(2,1)} %copy-done.3, ...), custom_call_target="tpu_custom_call" | custom-call | tf_op jit(solution)/shard_map/pallas_call | solution.py:88
  75.2 1.0 select_bitcast_fusion.2
  76.2 5.0 %collective-permute-start.5 = (bf16[32,16,74]{2,1,0:T(8,128)(2,1)S(1)}, bf16[32,16,74]{2,1,0:T(8,128)(2,1)S(1)}, u32[]{:S(2)}, u32[]{:S(2)}) collective-permute-start(bf16[32,16,74]{2,1,0:T(8,128)(2,1)S(1)} %select_bitcast_fusion.2), channel_id=1, source_target_pairs={{0,200},{8,192},{64,136},{72,128},{128,72},{136,64},{192,8},{200,0... | collective-permute-start | bytes 227336 | tf_op jit(solution)/shard_map/ppermute | solution.py:137
  81.1 1.4 collective-permute-done.7.s_ref
  83.2 3.3 %shard_map.36 = bf16[2,32,16,74]{3,2,1,0:T(8,128)(2,1)} custom-call(s32[2]{0:T(128)} %pad_add_fusion.q_ref, bf16[2,56,18944]{2,1,0:T(8,128)(2,1)} %a1.17, bf16[2,56,18944]{2,1,0:T(8,128)(2,1)} %f1.17, bf16[2,56,18944]{2,1,0:T(8,128)(2,1)} %a1.17, bf16[2,56,18944]{2,1,0:T(8,128)(2,1)} %f1.17, bf16[2,2,16,4736]{3,2,1,0:T(8,128)(2,1)} %copy-done.2, ...), custom_call_target="tpu_custom_call" | custom-call | tf_op jit(solution)/shard_map/pallas_call | solution.py:88
  86.6 1.0 select_bitcast_fusion.1
  87.6 10.3 %collective-permute-start.8 = (bf16[32,16,74]{2,1,0:T(8,128)(2,1)S(1)}, bf16[32,16,74]{2,1,0:T(8,128)(2,1)S(1)}, u32[]{:S(2)}, u32[]{:S(2)}) collective-permute-start(bf16[32,16,74]{2,1,0:T(8,128)(2,1)S(1)} %select_bitcast_fusion.1), channel_id=1, source_target_pairs={{0,200},{8,192},{64,136},{72,128},{128,72},{136,64},{192,8},{200,0... | collective-permute-start | bytes 227336 | tf_op jit(solution)/shard_map/ppermute | solution.py:137
  97.9 2.3 %collective-permute-done.5 = bf16[32,16,74]{2,1,0:T(8,128)(2,1)S(1)} collective-permute-done((bf16[32,16,74]{2,1,0:T(8,128)(2,1)S(1)}, bf16[32,16,74]{2,1,0:T(8,128)(2,1)S(1)}, u32[]{:S(2)}, u32[]{:S(2)}) %collective-permute-start.5) | collective-permute-done | bytes 75808 | tf_op jit(solution)/shard_map/ppermute | solution.py:137
  101.0 8.3 %all-to-all-start.1 = ((bf16[32,2,16,74]{3,2,1,0:T(8,128)(2,1)}), bf16[32,2,16,74]{3,2,1,0:T(8,128)(2,1)S(1)}, u32[]{:S(2)}, u32[]{:S(2)}) async-start(bf16[32,2,16,74]{3,2,1,0:T(8,128)(2,1)} %copy.7), calls=%async_computation.1 | async-start | bytes 524288 | tf_op jit(solution)/shard_map/all_to_all | solution.py:139
  109.4 0.8 copy-done.6
  110.1 4.6 %shard_map.30 = bf16[2,32,24,74]{3,2,1,0:T(8,128)(2,1)} custom-call(s32[2]{0:T(128)} %pad_add_fusion.q_ref, bf16[2,56,18944]{2,1,0:T(8,128)(2,1)} %a1.17, bf16[2,56,18944]{2,1,0:T(8,128)(2,1)} %f1.17, bf16[2,56,18944]{2,1,0:T(8,128)(2,1)} %a1.17, bf16[2,56,18944]{2,1,0:T(8,128)(2,1)} %f1.17, bf16[2,2,24,4736]{3,2,1,0:T(8,128)(2,1)} %copy-done, ...), custom_call_target="tpu_custom_call" | custom-call | tf_op jit(solution)/shard_map/pallas_call | solution.py:88
  114.8 1.1 select_bitcast_fusion
  115.8 5.4 %collective-permute-start.2 = (bf16[32,24,74]{2,1,0:T(8,128)(2,1)S(1)}, bf16[32,24,74]{2,1,0:T(8,128)(2,1)S(1)}, u32[]{:S(2)}, u32[]{:S(2)}) collective-permute-start(bf16[32,24,74]{2,1,0:T(8,128)(2,1)S(1)} %select_bitcast_fusion), channel_id=1, source_target_pairs={{0,200},{8,192},{64,136},{72,128},{128,72},{136,64},{192,8},{200,0... | collective-permute-start | bytes 341000 | tf_op jit(solution)/shard_map/ppermute | solution.py:137
  122.0 7.7 %all-to-all-start.2 = ((bf16[32,2,16,74]{3,2,1,0:T(8,128)(2,1)}), bf16[32,2,16,74]{3,2,1,0:T(8,128)(2,1)S(1)}, u32[]{:S(2)}, u32[]{:S(2)}) async-start(bf16[32,2,16,74]{3,2,1,0:T(8,128)(2,1)} %copy.8), calls=%async_computation.2 | async-start | bytes 524288 | tf_op jit(solution)/shard_map/all_to_all | solution.py:139
  129.9 8.7 %all-to-all-done.2 = bf16[32,2,16,74]{3,2,1,0:T(8,128)(2,1)S(1)} async-done(((bf16[32,2,16,74]{3,2,1,0:T(8,128)(2,1)}), bf16[32,2,16,74]{3,2,1,0:T(8,128)(2,1)S(1)}, u32[]{:S(2)}, u32[]{:S(2)}) %all-to-all-start.2) | async-done | bytes 151584 | tf_op jit(solution)/shard_map/all_to_all | solution.py:139
  138.5 13.7 %all_to_all.15 = bf16[32,2,24,74]{3,2,1,0:T(8,128)(2,1)S(1)} all-to-all(bf16[32,2,24,74]{3,2,1,0:T(8,128)(2,1)S(1)} %copy.6), channel_id=1, replica_groups=mesh['task'=4,'y'=4,'half'=2,'x'=4,'core'=2] {'y','x','core'}, dimensions={0} | all-to-all | bytes 454656 | tf_op jit(solution)/shard_map/all_to_all | solution.py:139
  152.5 1.2 copy.10
  (36 shorter events, 4.7 us)
Async XLA Ops:
  6.5 56.9 %collective-permute-start = (bf16[2,2,24,4736]{3,2,1,0:T(8,128)(2,1)}, bf16[2,2,24,4736]{3,2,1,0:T(8,128)(2,1)S(1)}, u32[]{:S(2)}, u32[]{:S(2)}) collective-permute-start(bf16[2,2,24,4736]{3,2,1,0:T(8,128)(2,1)} %shard_map.28), channel_id=1, source_target_pairs={{0,64},{64,0},{128,192},{192,128},{1,65},{65,1},{129,193},{193,129... | collective-permute-start | bytes 2727944 | tf_op jit(solution)/shard_map/ppermute | solution.py:124
  12.7 28.4 %collective-permute-start.3 = (bf16[2,2,16,4736]{3,2,1,0:T(8,128)(2,1)}, bf16[2,2,16,4736]{3,2,1,0:T(8,128)(2,1)S(1)}, u32[]{:S(2)}, u32[]{:S(2)}) collective-permute-start(bf16[2,2,16,4736]{3,2,1,0:T(8,128)(2,1)} %shard_map.31), channel_id=1, source_target_pairs={{0,64},{64,0},{128,192},{192,128},{1,65},{65,1},{129,193},{193,129... | collective-permute-start | bytes 1818632 | tf_op jit(solution)/shard_map/ppermute | solution.py:124
  17.2 41.7 %collective-permute-start.6 = (bf16[2,2,16,4736]{3,2,1,0:T(8,128)(2,1)}, bf16[2,2,16,4736]{3,2,1,0:T(8,128)(2,1)S(1)}, u32[]{:S(2)}, u32[]{:S(2)}) collective-permute-start(bf16[2,2,16,4736]{3,2,1,0:T(8,128)(2,1)} %shard_map.34), channel_id=1, source_target_pairs={{0,64},{64,0},{128,192},{192,128},{1,65},{65,1},{129,193},{193,129... | collective-permute-start | bytes 1818632 | tf_op jit(solution)/shard_map/ppermute | solution.py:124
  41.1 0.8 copy-start.3
  45.0 26.1 %collective-permute-start.4 = (bf16[2,16,4736]{2,1,0:T(8,128)(2,1)}, bf16[2,16,4736]{2,1,0:T(8,128)(2,1)S(1)}, u32[]{:S(2)}, u32[]{:S(2)}) collective-permute-start(bf16[2,16,4736]{2,1,0:T(8,128)(2,1)} %shard_map.32), channel_id=1, source_target_pairs={{0,128},{64,192},{128,0},{192,64},{1,129},{65,193},{129,1},{193,65... | collective-permute-start | bytes 909320 | tf_op jit(solution)/shard_map/ppermute | solution.py:129
  58.9 0.8 copy-start.2
  62.8 19.7 %collective-permute-start.7 = (bf16[2,16,4736]{2,1,0:T(8,128)(2,1)}, bf16[2,16,4736]{2,1,0:T(8,128)(2,1)S(1)}, u32[]{:S(2)}, u32[]{:S(2)}) collective-permute-start(bf16[2,16,4736]{2,1,0:T(8,128)(2,1)} %shard_map.35), channel_id=1, source_target_pairs={{0,128},{64,192},{128,0},{192,64},{1,129},{65,193},{129,1},{193,65... | collective-permute-start | bytes 909320 | tf_op jit(solution)/shard_map/ppermute | solution.py:129
  63.5 0.9 copy-start
  68.7 40.6 %collective-permute-start.1 = (bf16[2,24,4736]{2,1,0:T(8,128)(2,1)}, bf16[2,24,4736]{2,1,0:T(8,128)(2,1)S(1)}, u32[]{:S(2)}, u32[]{:S(2)}) collective-permute-start(bf16[2,24,4736]{2,1,0:T(8,128)(2,1)} %shard_map.29), channel_id=1, source_target_pairs={{0,128},{64,192},{128,0},{192,64},{1,129},{65,193},{129,1},{193,65... | collective-permute-start | bytes 1363976 | tf_op jit(solution)/shard_map/ppermute | solution.py:129
  71.1 0.7 copy-start.7
  76.2 24.0 %copy-start.5 = (bf16[2,32,16,74]{3,2,1,0:T(8,128)(2,1)S(1)}, bf16[2,32,16,74]{3,2,1,0:T(8,128)(2,1)}, u32[]{:S(2)}) copy-start(bf16[2,32,16,74]{3,2,1,0:T(8,128)(2,1)} %shard_map.33) | copy-start | bytes 454660
  76.2 24.0 %collective-permute-start.5 = (bf16[32,16,74]{2,1,0:T(8,128)(2,1)S(1)}, bf16[32,16,74]{2,1,0:T(8,128)(2,1)S(1)}, u32[]{:S(2)}, u32[]{:S(2)}) collective-permute-start(bf16[32,16,74]{2,1,0:T(8,128)(2,1)S(1)} %select_bitcast_fusion.2), channel_id=1, source_target_pairs={{0,200},{8,192},{64,136},{72,128},{128,72},{136,64},{192,8},{200,0... | collective-permute-start | bytes 227336 | tf_op jit(solution)/shard_map/ppermute | solution.py:137
  82.5 0.7 copy-start.8
  86.6 22.8 %copy-start.4 = (bf16[2,32,16,74]{3,2,1,0:T(8,128)(2,1)S(1)}, bf16[2,32,16,74]{3,2,1,0:T(8,128)(2,1)}, u32[]{:S(2)}) copy-start(bf16[2,32,16,74]{3,2,1,0:T(8,128)(2,1)} %shard_map.36) | copy-start | bytes 454660
  87.6 21.7 %collective-permute-start.8 = (bf16[32,16,74]{2,1,0:T(8,128)(2,1)S(1)}, bf16[32,16,74]{2,1,0:T(8,128)(2,1)S(1)}, u32[]{:S(2)}, u32[]{:S(2)}) collective-permute-start(bf16[32,16,74]{2,1,0:T(8,128)(2,1)S(1)} %select_bitcast_fusion.1), channel_id=1, source_target_pairs={{0,200},{8,192},{64,136},{72,128},{128,72},{136,64},{192,8},{200,0... | collective-permute-start | bytes 227336 | tf_op jit(solution)/shard_map/ppermute | solution.py:137
  101.0 21.0 %all-to-all-start.1 = ((bf16[32,2,16,74]{3,2,1,0:T(8,128)(2,1)}), bf16[32,2,16,74]{3,2,1,0:T(8,128)(2,1)S(1)}, u32[]{:S(2)}, u32[]{:S(2)}) async-start(bf16[32,2,16,74]{3,2,1,0:T(8,128)(2,1)} %copy.7), calls=%async_computation.1 | async-start | bytes 524288 | tf_op jit(solution)/shard_map/all_to_all | solution.py:139
  109.4 0.8 copy-start.6
  114.7 14.9 %copy-start.1 = (bf16[2,32,24,74]{3,2,1,0:T(8,128)(2,1)S(1)}, bf16[2,32,24,74]{3,2,1,0:T(8,128)(2,1)}, u32[]{:S(2)}) copy-start(bf16[2,32,24,74]{3,2,1,0:T(8,128)(2,1)} %shard_map.30) | copy-start | bytes 681988
  115.8 13.8 %collective-permute-start.2 = (bf16[32,24,74]{2,1,0:T(8,128)(2,1)S(1)}, bf16[32,24,74]{2,1,0:T(8,128)(2,1)S(1)}, u32[]{:S(2)}, u32[]{:S(2)}) collective-permute-start(bf16[32,24,74]{2,1,0:T(8,128)(2,1)S(1)} %select_bitcast_fusion), channel_id=1, source_target_pairs={{0,200},{8,192},{64,136},{72,128},{128,72},{136,64},{192,8},{200,0... | collective-permute-start | bytes 341000 | tf_op jit(solution)/shard_map/ppermute | solution.py:137
  122.0 16.5 %all-to-all-start.2 = ((bf16[32,2,16,74]{3,2,1,0:T(8,128)(2,1)}), bf16[32,2,16,74]{3,2,1,0:T(8,128)(2,1)S(1)}, u32[]{:S(2)}, u32[]{:S(2)}) async-start(bf16[32,2,16,74]{3,2,1,0:T(8,128)(2,1)} %copy.8), calls=%async_computation.2 | async-start | bytes 524288 | tf_op jit(solution)/shard_map/all_to_all | solution.py:139
